TPU v7x, 32 devices: a whole 2x2x4 slice. The times are simulated.
32 devices in a mesh: tab: 8 (over y, x, core), rep: 4 (over z).
Axes of the slice: x: 2, y: 2, z: 4, core: 2. Of those that a mesh axis runs over, the one named last changes fastest.
Arguments:
- pooled: bfloat16 [64, 4096, 128], P('tab', 'rep'), may hold values from -6 to 6
- widths: int32 [64], replicated, may hold values from 16 to 128, as said below
- placement: int32 [64], replicated, may hold values from 0 to 63, each once
- route: int32 [4, 1024], P('rep'), may hold values from 0 to 1023, each once within a row
- labels: int32 [4, 1024], P('rep'), may hold values 0 or 1
- proj: bfloat16 [64, 128, 32], replicated, may hold values from -0.5 to 0.5
- senet_in: float32 [64, 32], replicated, may hold values from -6 to 6
- senet_out: float32 [32, 64], replicated, may hold values from -1 to 1
- bilinear: float32 [32, 32], replicated, may hold values from -1 to 1
- w_first: bfloat16 [4096, 256], replicated, may hold values from -0.09375 to 0.09375
- w_second: bfloat16 [256, 256], replicated, may hold values from -0.75 to 0.75
- w_last: bfloat16 [256], replicated, may hold values from -0.375 to 0.375
Outputs:
- scores: float32 [4, 1024], P('rep', 'tab')
- d_pooled: bfloat16 [64, 4096, 128], P('tab', 'rep')
- d_proj: float32 [64, 128, 32], P('tab')
- d_senet_in: float32 [64, 32], replicated
- d_senet_out: float32 [32, 64], replicated
- d_bilinear: float32 [32, 32], replicated
- d_first: float32 [4096, 256], P('tab')
- d_second: float32 [256, 256], replicated
- d_last: float32 [256], replicated
Inputs may be any that keep to these rules, and one draw needn't show every extreme that they name: `widths`: each field's width is 128, 64, 32 or 16. `placement`: a permutation of the fields. `route`: each row is a permutation of 0 to 1023.
All inputs are finite; a program needn't handle non-finite values. No bound on the sum of `labels` on one device may be relied on, other than what follows from the above.
Results may differ from a plain program's by a relative error of at most 0.017.
Values may be sent and summed in bfloat16 or wider, within the bound.
No kernel may reach another device: no remote copies, remote signals or barrier semaphores. Data moves between devices by JAX's collectives and lax.ppermute only.
A program may use at most 64 MiB of HBM per device.

v0:
```python
import jax
import jax.numpy as jnp
from jax import lax
from jax.sharding import PartitionSpec as P

PRECISE = lax.Precision.HIGHEST


def silu_slope(pre_act):
    logistic = jax.nn.sigmoid(pre_act)
    return logistic * (1.0 + pre_act * (1.0 - logistic))


def bilinear_forward(fields_in, bilinear, factor):
    product = jnp.einsum("fnc,cd->fnd", fields_in, bilinear, precision=PRECISE)
    others = jnp.sum(fields_in, axis=0, keepdims=True) - fields_in
    return (product * others * factor, product, others)


def bilinear_backward(fields_in, product, others, upstream, bilinear, factor):
    d_product = upstream * others * factor
    d_others = upstream * product * factor
    d_fields = jnp.einsum("fnd,cd->fnc", d_product, bilinear, precision=PRECISE)
    d_fields = d_fields + jnp.sum(d_others, axis=0, keepdims=True) - d_others
    d_weight = jnp.einsum("fnc,fnd->cd", fields_in, d_product, precision=PRECISE)
    return (d_fields, d_weight)


def owner_pass(embeds, targets, senet_in, senet_out, bilinear, w_first, w_second, w_last):
    count = embeds.shape[0]
    width = embeds.shape[2]
    hidden = w_second.shape[0]
    factor = count ** (-0.5)
    first = w_first.reshape(2, count, width, hidden)
    dense = embeds.astype(jnp.float32)
    squeeze = jnp.mean(dense, axis=2)
    pre_one = jnp.einsum("fn,fr->rn", squeeze, senet_in, precision=PRECISE)
    act_one = jax.nn.silu(pre_one)
    pre_two = jnp.einsum("rn,rf->fn", act_one, senet_out, precision=PRECISE)
    weights = jax.nn.sigmoid(pre_two)
    scaled = weights[:, :, None] * dense
    plain_out, plain_prod, plain_rest = bilinear_forward(dense, bilinear, factor)
    scaled_out, scaled_prod, scaled_rest = bilinear_forward(scaled, bilinear, factor)
    joined = jnp.stack([plain_out, scaled_out]).astype(jnp.bfloat16)
    pre_hidden = jnp.einsum("kfnc,kfch->nh", joined, first, preferred_element_type=jnp.float32)
    hidden_one = jax.nn.silu(pre_hidden).astype(jnp.bfloat16)
    pre_second = jnp.dot(hidden_one, w_second, preferred_element_type=jnp.float32)
    hidden_two = jax.nn.silu(pre_second).astype(jnp.bfloat16)
    logits = jnp.dot(hidden_two, w_last, preferred_element_type=jnp.float32)
    grad_logit = jax.nn.sigmoid(logits) - targets
    d_last = jnp.dot(grad_logit, hidden_two.astype(jnp.float32), precision=PRECISE)
    last_wide = w_last.astype(jnp.float32)
    d_pre_two = (grad_logit[:, None] * last_wide[None, :] * silu_slope(pre_second)).astype(
        jnp.bfloat16
    )
    d_second = jnp.dot(hidden_one.T, d_pre_two, preferred_element_type=jnp.float32)
    back_two = jnp.dot(d_pre_two, w_second.T, preferred_element_type=jnp.float32)
    d_pre_one = (back_two * silu_slope(pre_hidden)).astype(jnp.bfloat16)
    d_first = jnp.einsum(
        "kfnc,nh->kfch", joined, d_pre_one, preferred_element_type=jnp.float32
    ).reshape(-1, hidden)
    d_joined = jnp.einsum("nh,kfch->kfnc", d_pre_one, first, preferred_element_type=jnp.float32)
    d_plain, d_bil_plain = bilinear_backward(
        dense, plain_prod, plain_rest, d_joined[0], bilinear, factor
    )
    d_scaled, d_bil_scaled = bilinear_backward(
        scaled, scaled_prod, scaled_rest, d_joined[1], bilinear, factor
    )
    d_weights = jnp.sum(d_scaled * dense, axis=2)
    d_pre_w = d_weights * weights * (1.0 - weights)
    d_senet_out = jnp.einsum("rn,fn->rf", act_one, d_pre_w, precision=PRECISE)
    d_act = jnp.einsum("fn,rf->rn", d_pre_w, senet_out, precision=PRECISE) * silu_slope(pre_one)
    d_senet_in = jnp.einsum("fn,rn->fr", squeeze, d_act, precision=PRECISE)
    d_squeeze = jnp.einsum("rn,fr->fn", d_act, senet_in, precision=PRECISE)
    d_embeds = d_plain + weights[:, :, None] * d_scaled + d_squeeze[:, :, None] / width
    small = (d_senet_in, d_senet_out, d_bil_plain + d_bil_scaled, d_second, d_last)
    return (logits, d_embeds.astype(jnp.bfloat16), small, d_first, joined, d_pre_one)


def shards(
    pooled,
    widths,
    placement,
    route,
    labels,
    proj,
    senet_in,
    senet_out,
    bilinear,
    w_first,
    w_second,
    w_last,
):
    tab_count = lax.axis_size("tab")
    tab_index = lax.axis_index("tab")
    local_count = pooled.shape[0]
    rep_rows = pooled.shape[1]
    padded = pooled.shape[2]
    field_count = placement.shape[0]
    owner_rows = rep_rows // tab_count
    field_ids = jnp.arange(field_count, dtype=jnp.int32)
    matches = placement[:, None] == field_ids[None, :]
    slot_width = jnp.sum(jnp.where(matches, widths[None, :], 0), axis=1)
    slot_mask = (jnp.arange(padded, dtype=jnp.int32)[None, :] < slot_width[:, None]).astype(
        jnp.bfloat16
    )
    inverse = jnp.zeros_like(placement).at[placement].set(field_ids)
    targets = lax.dynamic_slice_in_dim(labels[0], tab_index * owner_rows, owner_rows).astype(
        jnp.float32
    )
    first_slot = tab_index * local_count
    local_fields = lax.dynamic_slice_in_dim(placement, first_slot, local_count)
    local_mask = lax.dynamic_slice_in_dim(slot_mask, first_slot, local_count, 0)
    local_proj = jnp.take(proj, local_fields, axis=0)
    masked = pooled * local_mask[:, None, :]
    embed_local = jnp.einsum(
        "fnc,fcd->fnd", masked, local_proj, preferred_element_type=jnp.float32
    ).astype(jnp.bfloat16)
    embed_slot = lax.all_to_all(embed_local, "tab", split_axis=1, concat_axis=0, tiled=True)
    logits, d_embeds, small, d_first_part, joined, d_pre_one = owner_pass(
        embed_slot[inverse], targets, senet_in, senet_out, bilinear, w_first, w_second, w_last
    )
    d_slot = d_embeds[placement]
    d_local = lax.all_to_all(d_slot, "tab", split_axis=0, concat_axis=1, tiled=True)
    back = jnp.einsum("fnd,fcd->fnc", d_local, local_proj, preferred_element_type=jnp.float32)
    back = (back * local_mask[:, None, :]).astype(jnp.bfloat16)
    d_proj_part = jnp.einsum("fnc,fnd->fcd", masked, d_local, preferred_element_type=jnp.float32)
    d_proj = lax.psum(d_proj_part.astype(jnp.bfloat16), "rep").astype(jnp.float32)
    first_all = lax.psum_scatter(d_first_part, ("tab", "rep"), scatter_dimension=0, tiled=True)
    d_first = lax.all_gather(first_all.astype(jnp.bfloat16), "rep", axis=0, tiled=True).astype(
        first_all.dtype
    )
    part_in, part_out, part_bil, part_second, part_last = small
    d_senet_in, d_senet_out, d_bilinear, d_second, d_last = lax.psum(
        (part_in, part_out, part_bil, part_second, part_last), ("tab", "rep")
    )
    all_logits = lax.all_gather(logits, "tab", axis=0, tiled=True)
    wanted = lax.dynamic_slice_in_dim(route[0], tab_index * owner_rows, owner_rows)
    scores = jnp.take(all_logits, wanted)[None, :]
    return (scores, back, d_proj, d_senet_in, d_senet_out, d_bilinear, d_first, d_second, d_last)


def solution(mesh):
    placed = (
        P("tab", "rep", None),
        P(),
        P(),
        P("rep", None),
        P("rep", None),
        P(),
        P(),
        P(),
        P(),
        P(),
        P(),
        P(),
    )
    return jax.shard_map(
        shards,
        mesh=mesh,
        in_specs=placed,
        out_specs=(
            P("rep", "tab"),
            P("tab", "rep", None),
            P("tab", None, None),
            P(),
            P(),
            P(),
            P("tab", None),
            P(),
            P(),
        ),
        check_vma=False,
    )
```

profile of v0, /device:TPU:0, one launch (start us, length us, event | category | flops | bytes accessed | tf_op | source)
XLA Modules:
  0.0 254.4 jit_solution(10931208529390182150)
XLA Ops:
  9.9 1.6 gather_fusion
  11.5 2.4 fusion.15
  14.0 2.5 copy.54
  16.5 4.6 %reshape.143 = bf16[8,2,16384]{2,1,0:T(2,128)(2,1)} reshape(bf16[1024,8,32]{2,1,0:T(8,128)(2,1)} %bitcast.132) | data formatting | bytes 1048576
  21.0 5.2 %all-to-all-start = ((bf16[8,2,16384]{2,1,0:T(2,128)(2,1)}), bf16[8,2,16384]{2,1,0:T(2,128)(2,1)S(1)}, u32[]{:S(2)}, u32[]{:S(2)}) async-start(bf16[8,2,16384]{2,1,0:T(2,128)(2,1)} %reshape.143), calls=%async_computation | async-start | bytes 1048576 | tf_op jit(solution)/shard_map/all_to_all | solution.py:119
  27.3 8.6 %all-to-all-done = bf16[8,2,16384]{2,1,0:T(2,128)(2,1)S(1)} async-done(((bf16[8,2,16384]{2,1,0:T(2,128)(2,1)}), bf16[8,2,16384]{2,1,0:T(2,128)(2,1)S(1)}, u32[]{:S(2)}, u32[]{:S(2)}) %all-to-all-start) | async-done | bytes 524320 | tf_op jit(solution)/shard_map/all_to_all | solution.py:119
  35.9 2.0 reshape.144
  37.9 2.2 copy.56
  47.4 1.5 fusion.44
  49.4 1.5 fusion.14
  50.8 1.4 gather_fusion.3
  52.3 13.1 %all_to_all.36 = bf16[64,128,32]{1,2,0:T(8,128)(2,1)S(1)} all-to-all(bf16[64,128,32]{1,2,0:T(8,128)(2,1)} %gather_fusion.3), channel_id=1, replica_groups=mesh['tab'=8,'rep'=4] {'tab'}, dimensions={0} | all-to-all | bytes 1048576 | tf_op jit(solution)/shard_map/all_to_all | solution.py:124
  65.4 2.9 %fusion.25 = bf16[8,128,32]{1,2,0:T(8,128)(2,1)} fusion(bf16[8,1024,128]{2,1,0:T(8,128)(2,1)} %param.12, bf16[8,128]{1,0:T(8,128)(2,1)S(1)} %copy-done.11, bf16[8,8,4,8,128]{4,3,2,1,0:T(8,128)(2,1)S(1)} %bitcast.134), kind=kOutput, calls=%fused_computation.36 | convolution fusion | flops 71335936 | bytes 2689024 | tf_op jit(solution)/shard_map/fnc,fnd->fcd/dot_general | solution.py:127
  68.3 3.8 %fusion.107 = f32[2,64,32,256]{3,2,1,0:T(8,128)} fusion(bf16[128,256,1,1]{1,0,3,2:T(8,128)(2,1)S(1)} %fusion.29, bf16[1,64,128,32]{2,3,1,0:T(8,128)(2,1)} %copy-done.3, bf16[1,64,128,32]{2,3,1,0:T(8,128)(2,1)} %copy-done.2), kind=kOutput, calls=%fused_computation.145 | convolution fusion | flops 268959744 | bytes 5308416 | tf_op jit(solution)/shard_map/kfnc,nh->kfch/dot_general | solution.py:59
  72.9 8.0 %all-gather = f32[8,1,128]{2,1,0:T(1,128)S(1)} all-gather(f32[1,1,128]{2,1,0:T(1,128)S(1)} %bitcast.137), channel_id=1, replica_groups=mesh['tab'=8,'rep'=4] {'tab'}, dimensions={0}, use_global_device_ids=true | all-gather | bytes 4608 | tf_op jit(solution)/shard_map/all_gather | solution.py:137
  81.9 2.0 convolution_bitcast_fusion.1
  86.6 2.4 fusion.37
  89.1 41.4 %all-reduce = (f32[64,32]{0,1:T(8,128)}, f32[32,64]{1,0:T(8,128)}, f32[32,32]{1,0:T(8,128)}, f32[256]{0:T(256)}) all-reduce(f32[64,32]{0,1:T(8,128)S(1)} %fusion.71, f32[32,64]{1,0:T(8,128)S(1)} %fusion.82, f32[32,32]{1,0:T(8,128)S(1)} %fusion.37, f32[256]{0:T(256)S(1)} %bitcast.136), channel_id=1, replica_groups=mesh['tab'=8,'rep'=4] {'tab','rep'}, use_global_device_ids=true, to_apply=%region_9.10 | all-reduce | flops 5376 | bytes 43008 | tf_op jit(solution)/shard_map/psum | solution.py:134
  130.5 2.2 multiply_convert_fusion
  132.7 1.5 convert_element_type.68
  134.2 87.1 %reduce-scatter.2.cloned.1.call-done = f32[128,256]{1,0:T(8,128)} async-done(((f32[4096,256]{1,0:T(8,128)}), f32[128,256]{1,0:T(8,128)}) %reduce-scatter.2.cloned.1.call-update) | async-done | bytes 131088 | tf_op jit(solution)/shard_map/reduce_scatter | solution.py:129
  222.2 14.3 %all_gather.7 = bf16[512,256]{1,0:T(8,128)(2,1)S(1)} all-gather(bf16[128,256]{1,0:T(8,128)(2,1)S(1)} %convert_element_type.69), channel_id=1, replica_groups=mesh['tab'=8,'rep'=4] {'rep'}, dimensions={0}, use_global_device_ids=true | all-gather | bytes 327680 | tf_op jit(solution)/shard_map/all_gather | solution.py:130
  237.3 8.0 %all-reduce.6.cloned.1.call-done = f32[256,256]{1,0:T(8,128)} async-done(((f32[256,256]{1,0:T(8,128)}), f32[256,256]{1,0:T(8,128)}) %all-reduce.6.cloned.1.call-update) | async-done | bytes 262160 | tf_op jit(solution)/shard_map/psum | solution.py:134
  245.3 1.7 copy.91
  (88 shorter events, 16.6 us)
Async XLA Ops:
  8.0 35.7 %copy-start = (bf16[4096,256]{1,0:T(8,128)(2,1)S(1)}, bf16[4096,256]{1,0:T(8,128)(2,1)}, u32[]{:S(2)}) copy-start(bf16[4096,256]{1,0:T(8,128)(2,1)} %param.21) | copy-start | bytes 6291460
  9.8 6.7 %copy-start.8 = (pred[8]{0:T(512)(128)(4,1)}, pred[8]{0:T(512)(128)(4,1)S(1)}, u32[]{:S(2)}) copy-start(pred[8]{0:T(512)(128)(4,1)S(1)} %get-tuple-element.17) | copy-start | bytes 28
  9.9 6.5 %copy-start.10 = (bf16[8,128]{1,0:T(8,128)(2,1)}, bf16[8,128]{1,0:T(8,128)(2,1)S(1)}, u32[]{:S(2)}) copy-start(bf16[8,128]{1,0:T(8,128)(2,1)S(1)} %get-tuple-element.22) | copy-start | bytes 6148
  16.5 9.8 %copy-start.12 = (s32[64]{0:T(128)S(1)}, s32[64]{0:T(128)}, u32[]{:S(2)}) copy-start(s32[64]{0:T(128)} %param.14) | copy-start | bytes 772
  16.5 9.8 %copy-start.14 = (bf16[256]{0:T(256)(128)(2,1)S(1)}, bf16[256]{0:T(256)(128)(2,1)}, u32[]{:S(2)}) copy-start(bf16[256]{0:T(256)(128)(2,1)} %param.23) | copy-start | bytes 1540
  21.0 14.9 %all-to-all-start = ((bf16[8,2,16384]{2,1,0:T(2,128)(2,1)}), bf16[8,2,16384]{2,1,0:T(2,128)(2,1)S(1)}, u32[]{:S(2)}, u32[]{:S(2)}) async-start(bf16[8,2,16384]{2,1,0:T(2,128)(2,1)} %reshape.143), calls=%async_computation | async-start | bytes 1048576 | tf_op jit(solution)/shard_map/all_to_all | solution.py:119
  26.2 106.5 %all-reduce.4.cloned.1.call-start = ((), (), s32[]{:S(2)}) async-start(), calls=%async_computation.3 | async-start | bytes 131072 | tf_op jit(solution)/shard_map/psum | solution.py:128
  26.3 19.6 %copy-start.15 = (f32[256]{0:T(256)}, f32[256]{0:T(256)S(1)}, u32[]{:S(2)}) copy-start(f32[256]{0:T(256)S(1)} %convert_element_type.61) | copy-start | bytes 3076
  40.1 0.8 copy-start.5
  40.1 1.0 copy-start.6
  40.2 1.4 copy-start.4
  43.7 1.0 copy-start.3
  43.7 1.1 copy-start.13
  44.8 2.0 copy-start.17
  45.0 1.8 copy-start.19
  46.9 2.5 copy-start.1
  47.4 1.5 copy-start.7
  50.8 14.5 %copy-start.11 = (bf16[8,128]{1,0:T(8,128)(2,1)S(1)}, bf16[8,128]{1,0:T(8,128)(2,1)}, u32[]{:S(2)}) copy-start(bf16[8,128]{1,0:T(8,128)(2,1)} %copy-done.10) | copy-start | bytes 6148
  68.3 153.0 %reduce-scatter.2.cloned.1.call-start = ((), (), s32[]{:S(2)}) async-start(), calls=%async_computation.4 | async-start | bytes 4325376 | tf_op jit(solution)/shard_map/reduce_scatter | solution.py:129
  72.2 13.5 %copy-start.16 = (f32[256]{0:T(256)S(1)}, f32[256]{0:T(256)}, u32[]{:S(2)}) copy-start(f32[256]{0:T(256)} %copy-done.15) | copy-start | bytes 3076
  72.2 173.1 %all-reduce.6.cloned.1.call-start = ((), (), s32[]{:S(2)}) async-start(), calls=%async_computation.5 | async-start | bytes 524288 | tf_op jit(solution)/shard_map/psum | solution.py:134
  81.9 3.8 %copy-start.18 = (f32[128,256]{1,0:T(8,128)S(1)}, f32[128,256]{1,0:T(8,128)}, u32[]{:S(2)}) copy-start(f32[128,256]{1,0:T(8,128)} %copy-done.17) | copy-start | bytes 393220
  81.9 3.7 %copy-start.20 = (f32[128,256]{1,0:T(8,128)S(1)}, f32[128,256]{1,0:T(8,128)}, u32[]{:S(2)}) copy-start(f32[128,256]{1,0:T(8,128)} %copy-done.19) | copy-start | bytes 393220
  84.0 46.6 %copy-start.9 = (pred[8]{0:T(512)(128)(4,1)S(1)}, pred[8]{0:T(512)(128)(4,1)}, u32[]{:S(2)}) copy-start(pred[8]{0:T(512)(128)(4,1)} %copy-done.8) | copy-start | bytes 28
  (1 other events, 0.8 us)
Sparse Core Ops, SparseCore 0:
  68.4 37.1 all-reduce.3
  111.7 133.5 all-reduce.5
Sparse Core Ops, SparseCore 1:
  72.3 149.0 reduce-scatter.1
where the time goes:
time: 255 us; the launch traced here: 254 us
  waiting for transfers between devices  104 us (41%)
  blocking collectives  76.9 us (30%)
  matrix products  25.2 us (10%)
  local copies, waits for them, and re-layouts  19.2 us (8%)
  between operations  16 us (6%)
  other arithmetic  8.18 us (3%)
  starting transfers between devices  5.32 us (2%)
    reduce_scatter x1, waiting for transfers between devices, shards(): lax.psum_scatter(d_first_part, ('tab', 'rep'), scatter_dimension=0, tiled...  87.1 us
    psum x1, blocking collectives, shards(): lax.psum((part_in, part_out, part_bil, part_second, part_last), ('tab', '...  41.4 us
    all_gather x1, blocking collectives, shards(): lax.all_gather(first_all.astype(jnp.bfloat16), 'rep', axis=0, tiled=True)  14.3 us
    all_to_all x1, blocking collectives, shards(): lax.all_to_all(d_slot, 'tab', split_axis=0, concat_axis=1, tiled=True)  13.1 us
    unnamed x46, local copies, waits for them, and re-layouts  8.85 us
    all_to_all x1, waiting for transfers between devices, shards(): lax.all_to_all(embed_local, 'tab', split_axis=1, concat_axis=0, tiled=True)  8.59 us
    all_gather x1, blocking collectives, shards(): all_logits = lax.all_gather(logits, 'tab', axis=0, tiled=True)  8.03 us
    psum x1, waiting for transfers between devices, shards(): lax.psum((part_in, part_out, part_bil, part_second, part_last), ('tab', '...  7.97 us
  transfers between devices with their start and end apart: 4, of which 3 were waited for; matrix products, arithmetic and copies ran while one was open for 7% of the time, Pallas kernels for 0%

commit v1 on v0

v1 whole, which is shorter than its diff:
```python
import functools

import jax
import jax.numpy as jnp
from jax import lax
from jax.experimental import pallas as pl
from jax.experimental.pallas import tpu as pltpu
from jax.sharding import PartitionSpec as P


PRECISE = lax.Precision.HIGHEST
BF = jnp.bfloat16
F32 = jnp.float32
VMEM = pltpu.VMEM
NN = (((1,), (0,)), ((), ()))
NT = (((1,), (1,)), ((), ()))
TN = (((0,), (0,)), ((), ()))


def dot(a, b, dims=NN, precision=None):
    return lax.dot_general(a, b, dims, precision=precision, preferred_element_type=F32)


def split(x):
    high = x.astype(BF)
    return high, (x - high.astype(F32)).astype(BF)


def silu_slope(pre_act):
    logistic = jax.nn.sigmoid(pre_act)
    return logistic * (1.0 + pre_act * (1.0 - logistic))


def vspec():
    return pl.BlockSpec(memory_space=VMEM)


def hspec():
    return pl.BlockSpec(memory_space=pltpu.HBM)


def far(*arrays):
    return tuple(pltpu.with_memory_space_constraint(a, pltpu.HBM) for a in arrays)


def params(mebibytes):
    return pltpu.CompilerParams(vmem_limit_bytes=mebibytes << 20)


def embed_body(widths_hbm, placement_hbm, pooled, proj, out, weight_out, widths, placement, rows_in, gathered, weights, staged, sems, table_sems, out_sems):
    slots, _, padded = rows_in.shape
    width = proj.shape[1]
    tab, _, owner = staged.shape
    first = lax.axis_index("tab") * slots
    tables = [
        pltpu.make_async_copy(placement_hbm, placement, table_sems.at[0]),
        pltpu.make_async_copy(widths_hbm, widths, table_sems.at[1]),
    ]
    for copy in tables:
        copy.start()
    large = [pltpu.make_async_copy(pooled.at[s], rows_in.at[s], sems.at[0, s]) for s in range(slots)]
    for copy in large:
        copy.start()
    for copy in tables:
        copy.wait()
    small = [pltpu.make_async_copy(proj.at[placement[first + s]], gathered.at[s], sems.at[1, s]) for s in range(slots)]
    for copy in small:
        copy.start()
    lane = lax.broadcasted_iota(jnp.int32, (width, padded), 1)
    gone = []
    for s in range(slots):
        part = slice(s * width, (s + 1) * width)
        keep = lane < widths[placement[first + s]]
        small[s].wait()
        weight = jnp.where(keep, gathered[s].astype(F32), 0.0).astype(BF)
        weights[part, :] = weight
        large[s].wait()
        embeds = dot(weight, rows_in[s], NT).astype(BF)
        for o in range(tab):
            staged[o, part, :] = embeds[:, o * owner : (o + 1) * owner]
        copy = pltpu.make_async_copy(staged.at[:, part, :], out.at[:, part, :], out_sems.at[s])
        copy.start()
        gone.append(copy)
    copy = pltpu.make_async_copy(weights, weight_out, table_sems.at[0])
    copy.start()
    gone.append(copy)
    for copy in gone:
        copy.wait()


def embed_slots(widths, placement, pooled, proj, tab):
    slots, rows, padded = pooled.shape
    width = proj.shape[1]
    fields = placement.shape[0]
    return pl.pallas_call(
        embed_body,
        out_shape=(
            pltpu.HBM((tab, slots * width, rows // tab), BF),
            pltpu.HBM((slots * width, padded), BF),
        ),
        in_specs=[hspec()] * 4,
        out_specs=(hspec(), hspec()),
        scratch_shapes=[
            pltpu.SMEM((fields,), jnp.int32),
            pltpu.SMEM((fields,), jnp.int32),
            pltpu.VMEM((slots, rows, padded), BF),
            pltpu.VMEM((slots, width, padded), BF),
            pltpu.VMEM((slots * width, padded), BF),
            pltpu.VMEM((tab, slots * width, rows // tab), BF),
            pltpu.SemaphoreType.DMA((2, slots)),
            pltpu.SemaphoreType.DMA((2,)),
            pltpu.SemaphoreType.DMA((slots,)),
        ],
        compiler_params=params(12),
        name="embed_slots",
    )(*far(widths, placement, pooled, proj))


def prepare_body(order, first_hbm, second_hbm, bilinear_hbm, last_hbm, *rest):
    outs, (first, second, bilinear, last), made, sems, out_sems = rest[:6], rest[6:10], rest[10:16], rest[16], rest[17]
    first_turned, second_turned, kron_high, kron_low, back_high, last_column = made
    copies = [
        pltpu.make_async_copy(source, target, sems.at[i])
        for i, (source, target) in enumerate(
            ((bilinear_hbm, bilinear), (last_hbm, last), (second_hbm, second), (first_hbm, first))
        )
    ]
    for copy in copies:
        copy.start()
    leaving = [pltpu.make_async_copy(made[i], outs[i], out_sems.at[i]) for i in range(len(outs))]
    width = bilinear.shape[0]
    side = kron_high.shape[0]
    copies[0].wait()
    tiled = jnp.concatenate([bilinear[...]] * (side // width), axis=1)
    tiled = jnp.concatenate([tiled] * (side // width), axis=0)
    row = lax.broadcasted_iota(jnp.int32, (side, side), 0) // width
    column = lax.broadcasted_iota(jnp.int32, (side, side), 1) // width
    kron = jnp.where(row == column, tiled, 0.0)
    back_high[...] = kron.astype(BF)
    kron_high[...], kron_low[...] = split(kron.T)
    hidden = last.shape[1]
    row = lax.broadcasted_iota(jnp.int32, (hidden, hidden), 0)
    column = lax.broadcasted_iota(jnp.int32, (hidden, hidden), 1)
    copies[1].wait()
    last_column[...] = jnp.sum(jnp.where(row == column, last[...].astype(F32), 0.0), axis=1, keepdims=True)
    copies[2].wait()
    second_turned[...] = second[...].T
    for copy in leaving[1:]:
        copy.start()
    copies[3].wait()
    step = min(512, first.shape[0])
    for g in range(0, first.shape[0], step):
        first_turned[:, g : g + step] = first[g : g + step, :].T
    leaving[0].start()
    for copy in leaving:
        copy.wait()


def prepare(order, w_first, w_second, bilinear, w_last):
    total, hidden = w_first.shape
    side = min(256, total)
    shapes = (
        ((hidden, total), BF), ((hidden, hidden), BF), ((side, side), BF), ((side, side), BF), ((side, side), BF),
        ((hidden, 1), F32),
    )
    return pl.pallas_call(
        prepare_body,
        out_shape=tuple(pltpu.HBM(s, d) for s, d in shapes),
        in_specs=[hspec()] * 5,
        out_specs=tuple(hspec() for _ in shapes),
        scratch_shapes=[
            pltpu.VMEM(w_first.shape, BF),
            pltpu.VMEM(w_second.shape, BF),
            pltpu.VMEM(bilinear.shape, F32),
            pltpu.VMEM(w_last.shape, BF),
            *[pltpu.VMEM(s, d) for s, d in shapes],
            pltpu.SemaphoreType.DMA((4,)),
            pltpu.SemaphoreType.DMA((len(shapes),)),
        ],
        compiler_params=params(12),
        name="prepare",
    )(*far(order, w_first, w_second, bilinear, w_last))


def owner_body(placement_hbm, *refs):
    count = 12
    sources, (kept_hbm, moved_hbm, send_hbm) = refs[:count], refs[count : count + 3]
    placement = refs[count + 3]
    loaded = refs[count + 4 : 2 * count + 4]
    kept, moved, send, embeds_ref, product_ref, grad_ref, flat, sems, out_sems = refs[2 * count + 4 :]
    arrived, labels, senet_in, senet_out, kron_high, kron_low, first_turned, second_turned, last, second, back_high, first = loaded
    tables = pltpu.make_async_copy(placement_hbm, placement, sems.at[count])
    tables.start()
    loads = [pltpu.make_async_copy(sources[i], loaded[i], sems.at[i]) for i in range(count)]
    for copy in loads:
        copy.start()

    fields = placement.shape[0]
    total, lanes = arrived.shape
    width = total // fields
    factor = fields ** -0.5
    chunk = kron_high.shape[0]
    per = chunk // width
    chips, rows, _ = kept.shape
    step = min(chunk, rows)
    hidden = second.shape[0]
    mine = lax.axis_index("tab")
    core = mine % 2
    tables.wait()
    loads[0].wait()
    for s in range(fields):
        spot = pl.multiple_of(placement[s] * width, width)
        embeds_ref[pl.ds(spot, width), :] = arrived[s * width : (s + 1) * width, :]

    dense3 = embeds_ref[...].astype(F32).reshape(fields, width, lanes)
    squeeze = jnp.sum(dense3, axis=1) * (1.0 / width)
    for copy in loads[1:6]:
        copy.wait()
    pre_one = dot(senet_in[...], squeeze, NN, PRECISE)
    act_one = pre_one * jax.nn.sigmoid(pre_one)
    weights = jax.nn.sigmoid(dot(senet_out[...], act_one, TN, PRECISE))
    sum_plain = jnp.zeros((width, lanes), F32)
    sum_scaled = jnp.zeros((width, lanes), F32)
    for f in range(fields):
        one = embeds_ref[f * width : (f + 1) * width, :].astype(F32)
        sum_plain = sum_plain + one
        sum_scaled = sum_scaled + one * weights[f : f + 1, :]
    loads[6].wait()
    pre_hidden = jnp.zeros((hidden, lanes), F32)
    for g in range(0, total, chunk):
        block = embeds_ref[g : g + chunk, :]
        product = dot(kron_high[...], block) + dot(kron_low[...], block)
        product_ref[g : g + chunk, :] = product
        product3 = product.reshape(per, width, lanes) * factor
        dense = block.astype(F32).reshape(per, width, lanes)
        scale = weights[g // width : g // width + per][:, None, :]
        plain = (product3 * (sum_plain[None] - dense)).reshape(chunk, lanes).astype(BF)
        scaled = (product3 * scale * (sum_scaled[None] - dense * scale)).reshape(chunk, lanes).astype(BF)
        for start, values in ((g, plain), (total + g, scaled)):
            pre_hidden = pre_hidden + dot(first_turned[:, start : start + chunk], values)
            for piece in range(0, chunk, step):
                owner, spot = divmod(start + piece, rows)
                part = values[piece : piece + step]

                @pl.when(core == owner % 2)
                def _():
                    kept[owner // 2, spot : spot + step, :] = part

                @pl.when(core != owner % 2)
                def _():
                    moved[owner // 2 * rows + spot : owner // 2 * rows + spot + step, :] = part

    leave_kept = pltpu.make_async_copy(kept, kept_hbm, out_sems.at[0])
    leave_kept.start()
    for copy in loads[7:]:
        copy.wait()
    hidden_one = (pre_hidden * jax.nn.sigmoid(pre_hidden)).astype(BF)
    pre_second = dot(second_turned[...], hidden_one)
    hidden_two = (pre_second * jax.nn.sigmoid(pre_second)).astype(BF)
    hidden_wide = hidden_two.astype(F32)
    last_wide = last[...]
    logits = jnp.sum(last_wide * hidden_wide, axis=0, keepdims=True)
    grad_logit = jax.nn.sigmoid(logits) - labels[pl.ds(mine, 1), :].astype(F32)
    d_last = jnp.sum(hidden_wide * grad_logit, axis=1, keepdims=True)
    d_pre_two = (grad_logit * last_wide * silu_slope(pre_second)).astype(BF)
    flat[:hidden, :] = dot(hidden_one, d_pre_two, NT)
    d_pre_one = (dot(second[...], d_pre_two) * silu_slope(pre_hidden)).astype(BF)
    moved[chips * rows :, :] = d_pre_one
    leave_moved = pltpu.make_async_copy(moved, moved_hbm, out_sems.at[1])
    leave_moved.start()

    rest_plain = jnp.zeros((width, lanes), F32)
    rest_scaled = jnp.zeros((width, lanes), F32)
    bil = jnp.zeros((chunk, chunk), F32)
    d_weight_parts = []
    for g in range(0, total, chunk):
        d_plain = dot(first[g : g + chunk, :], d_pre_one).reshape(per, width, lanes)
        d_scaled = dot(first[total + g : total + g + chunk, :], d_pre_one).reshape(per, width, lanes)
        block = embeds_ref[g : g + chunk, :]
        dense = block.astype(F32).reshape(per, width, lanes)
        scale = weights[g // width : g // width + per][:, None, :]
        product = product_ref[g : g + chunk, :].reshape(per, width, lanes) * factor
        others_scaled = d_scaled * product
        d_others_plain = d_plain * product
        d_others_scaled = others_scaled * scale
        rest_plain = rest_plain + jnp.sum(d_others_plain, axis=0)
        rest_scaled = rest_scaled + jnp.sum(d_others_scaled, axis=0)
        away_scaled = sum_scaled[None] - dense * scale
        d_product = (d_plain * (sum_plain[None] - dense) + d_scaled * scale * away_scaled) * factor
        direct = d_product.reshape(chunk, lanes).astype(BF)
        bil = bil + dot(block, direct, NT)
        back = dot(back_high[...], direct).reshape(per, width, lanes)
        grad = back - d_others_plain - d_others_scaled * scale
        grad_ref[g : g + chunk, :] = grad.reshape(chunk, lanes)
        d_weight_parts.append(jnp.sum(others_scaled * away_scaled - dense * d_others_scaled, axis=1))
    d_bil = bil[0:width, 0:width]
    for i in range(1, per):
        d_bil = d_bil + bil[i * width : (i + 1) * width, i * width : (i + 1) * width]
    dense3 = embeds_ref[...].astype(F32).reshape(fields, width, lanes)
    d_weights = jnp.concatenate(d_weight_parts, axis=0) + jnp.sum(dense3 * rest_scaled[None], axis=1)
    d_pre_w = d_weights * weights * (1.0 - weights)
    d_out = dot(act_one, d_pre_w, NT, PRECISE)
    d_act = dot(senet_out[...], d_pre_w, NN, PRECISE) * silu_slope(pre_one)
    d_in = dot(d_act, squeeze, NT, PRECISE)
    d_squeeze = dot(senet_in[...], d_act, TN, PRECISE) * (1.0 / width)
    total_grad = (
        grad_ref[...].reshape(fields, width, lanes)
        + rest_plain[None]
        + weights[:, None, :] * rest_scaled[None]
        + d_squeeze[:, None, :]
    )
    grad_ref[...] = total_grad.reshape(total, lanes)
    tab, depth, _ = send.shape
    slots = fields // tab
    for s in range(fields):
        spot = pl.multiple_of(placement[s] * width, width)
        at = s % slots * width
        send[s // slots, at : at + width, :] = grad_ref[pl.ds(spot, width), :].astype(BF)
    senet = senet_in.shape[0]
    lines = flat.shape[0] // tab
    columns = [d_in, d_out, d_bil] + [d_last[i : i + senet, :] for i in range(0, hidden, senet)]
    used = sum(c.shape[1] for c in columns)
    flat[hidden:, :] = jnp.zeros((flat.shape[0] - hidden, hidden), F32)
    flat[hidden : hidden + senet, :] = jnp.concatenate(columns + [jnp.zeros((senet, hidden - used), F32)], axis=1)
    high = logits.astype(BF).astype(F32)
    base = slots * width
    spare = jnp.zeros((depth - base - hidden // lanes * lines - 2, lanes), F32)
    for t in range(tab):
        band = flat[t * lines : (t + 1) * lines, :]
        pieces = [band[:, i : i + lanes] for i in range(0, hidden, lanes)] + [high, logits - high, spare]
        send[t, base:, :] = jnp.concatenate(pieces, axis=0).astype(BF)
    leave_send = pltpu.make_async_copy(send, send_hbm, out_sems.at[2])
    leave_send.start()
    leave_kept.wait()
    leave_moved.wait()
    leave_send.wait()


def depth_of(base, lines, hidden, lanes):
    return -(-(base + hidden // lanes * lines + 2) // 16) * 16


def owner_pass(placement, arrived, labels, senet_in, senet_out, kron_high, kron_low, first_turned, second_turned, last, w_second, back_high, w_first):
    total, lanes = arrived.shape
    senet, fields = senet_in.shape
    hidden = w_second.shape[0]
    tab = labels.shape[0]
    rows = 2 * total // tab
    lines = -(-(hidden + senet) // tab)
    depth = depth_of(total // tab, lines, hidden, lanes)
    shapes = (((tab // 2, rows, lanes), BF), ((total + hidden, lanes), BF), ((tab, depth, lanes), BF))
    operands = (arrived, labels, senet_in, senet_out, kron_high, kron_low, first_turned, second_turned, last, w_second, back_high, w_first)
    return pl.pallas_call(
        owner_body,
        out_shape=tuple(pltpu.HBM(s, d) for s, d in shapes),
        in_specs=[hspec()] * (1 + len(operands)),
        out_specs=tuple(hspec() for _ in shapes),
        scratch_shapes=[
            pltpu.SMEM((fields,), jnp.int32),
            *[pltpu.VMEM(o.shape, o.dtype) for o in operands],
            *[pltpu.VMEM(s, d) for s, d in shapes],
            pltpu.VMEM((total, lanes), BF),
            pltpu.VMEM((total, lanes), F32),
            pltpu.VMEM((total, lanes), F32),
            pltpu.VMEM((lines * tab, hidden), F32),
            pltpu.SemaphoreType.DMA((len(operands) + 1,)),
            pltpu.SemaphoreType.DMA((3,)),
        ],
        compiler_params=params(24),
        name="owner_pass",
    )(*far(placement), arrived, *far(*operands[1:]))


def first_body(kept_hbm, moved_hbm, came_hbm, *rest):
    kept, moved, came, made, sems, out_sems = rest[-6:]
    outs = rest[:-6]
    chips, rows, _ = kept.shape
    chip = lax.axis_index("tab") // 2
    hidden = moved.shape[0]
    tail = pl.ds(chips * rows, hidden)
    heads = [
        pltpu.make_async_copy(moved_hbm.at[tail], moved, sems.at[0]),
        pltpu.make_async_copy(came_hbm.at[tail], came.at[tail], sems.at[1]),
    ]
    for copy in heads:
        copy.start()
    order = list(range(1, chips)) + [0]
    bodies = {}
    for q in order:
        target = chip ^ q
        part = pl.ds(pl.multiple_of(target * rows, rows), rows)
        bodies[q] = (
            pltpu.make_async_copy(kept_hbm.at[target], kept.at[q], sems.at[2 + 2 * q]),
            pltpu.make_async_copy(came_hbm.at[part], came.at[pl.ds(q * rows, rows)], sems.at[3 + 2 * q]),
        )
        for copy in bodies[q]:
            copy.start()
    for copy in heads:
        copy.wait()
    right = jnp.concatenate([moved[...], came[chips * rows :, :]], axis=1)
    gone = []
    for q in order:
        for copy in bodies[q]:
            copy.wait()
        left = jnp.concatenate([kept[q], came[q * rows : (q + 1) * rows, :]], axis=1)
        made[q] = dot(left, right, NT).astype(BF)
        copy = pltpu.make_async_copy(made.at[q], outs[q], out_sems.at[q])
        copy.start()
        gone.append(copy)
    for copy in gone:
        copy.wait()


def first_grad(kept, moved, came):
    chips, rows, lanes = kept.shape
    hidden = moved.shape[0] - chips * rows
    return pl.pallas_call(
        first_body,
        out_shape=tuple(pltpu.HBM((rows, hidden), BF) for _ in range(chips)),
        in_specs=[hspec()] * 3,
        out_specs=tuple(hspec() for _ in range(chips)),
        scratch_shapes=[
            pltpu.VMEM(kept.shape, BF),
            pltpu.VMEM((hidden, lanes), BF),
            pltpu.VMEM(came.shape, BF),
            pltpu.VMEM((chips, rows, hidden), BF),
            pltpu.SemaphoreType.DMA((2 + 2 * chips,)),
            pltpu.SemaphoreType.DMA((chips,)),
        ],
        compiler_params=params(8),
        name="first_grad",
    )(*far(kept, moved), came)


def tab_body(grads_any, route, summed_out, scores, grads, sem, *, base, line):
    tab, depth, owner = grads.shape
    copy = pltpu.make_async_copy(grads_any.at[:, pl.ds(base, depth), :], grads, sem)
    copy.start()
    wanted = route[pl.ds(lax.axis_index("tab"), 1), :]
    spot = lax.broadcasted_iota(jnp.int32, (owner, owner), 0)
    copy.wait()
    small = grads[0].astype(F32)
    for o in range(1, tab):
        small = small + grads[o].astype(F32)
    summed_out[...] = small.astype(BF)
    found = jnp.zeros((2, owner), F32)
    for o in range(tab):
        found = found + dot(grads[o, line : line + 2, :], (spot + o * owner == wanted).astype(F32).astype(BF))
    scores[...] = found[0:1] + found[1:2]


def tab_sums(grads, route, base, line):
    tab, depth, owner = grads.shape
    return pl.pallas_call(
        functools.partial(tab_body, base=base, line=line),
        out_shape=(
            jax.ShapeDtypeStruct((depth - base, owner), BF),
            jax.ShapeDtypeStruct((1, owner), F32),
        ),
        in_specs=[hspec(), vspec()],
        out_specs=(vspec(), vspec()),
        scratch_shapes=[pltpu.VMEM((tab, depth - base, owner), BF), pltpu.SemaphoreType.DMA(())],
        compiler_params=params(4),
        name="tab_sums",
    )(grads, route)


def slot_body(
    widths_hbm, placement_hbm, pooled, weight_hbm, grads_any, d_pooled, d_proj_hbm,
    widths, placement, rows_in, weight, grads, made, spread, d_proj, sems, in_sems, out_sems,
):
    slots, _, padded = rows_in.shape
    tab, total, owner = grads.shape
    width = total // slots
    first = lax.axis_index("tab") * slots
    pairs = (
        (grads_any.at[:, pl.ds(0, total), :], grads), (weight_hbm, weight), (placement_hbm, placement), (widths_hbm, widths),
    )
    copies = [pltpu.make_async_copy(source, target, sems.at[i]) for i, (source, target) in enumerate(pairs)]
    large = [pltpu.make_async_copy(pooled.at[s], rows_in.at[s], in_sems.at[s]) for s in range(slots)]
    for copy in copies + large:
        copy.start()
    spread[...] = jnp.zeros(spread.shape, BF)
    for copy in copies:
        copy.wait()
    for s in range(slots):
        spread[s * width : (s + 1) * width, s * padded : (s + 1) * padded] = weight[s * width : (s + 1) * width, :]
    gone = []
    for o in range(tab):
        part = slice(o * owner, (o + 1) * owner)
        back = dot(grads[o], spread[...], TN).astype(BF)
        for s in range(slots):
            made[s, part, :] = back[:, s * padded : (s + 1) * padded]
        copy = pltpu.make_async_copy(made.at[:, part, :], d_pooled.at[:, part, :], out_sems.at[o])
        copy.start()
        gone.append(copy)
    lane = lax.broadcasted_iota(jnp.int32, (width, padded), 1)
    for s in range(slots):
        left = jnp.concatenate([grads[o, s * width : (s + 1) * width, :] for o in range(tab)], axis=1)
        keep = lane < widths[placement[first + s]]
        large[s].wait()
        d_proj[s * width : (s + 1) * width, :] = jnp.where(keep, dot(left, rows_in[s]), 0.0).astype(BF)
    copy = pltpu.make_async_copy(d_proj, d_proj_hbm, sems.at[0])
    copy.start()
    gone.append(copy)
    for copy in gone:
        copy.wait()


def slot_grad(widths, placement, pooled, weight, grads):
    slots, _, padded = pooled.shape
    total = weight.shape[0]
    fields = placement.shape[0]
    tab, _, owner = grads.shape
    return pl.pallas_call(
        slot_body,
        out_shape=(pltpu.HBM(pooled.shape, BF), pltpu.HBM((total, padded), BF)),
        in_specs=[hspec()] * 5,
        out_specs=(hspec(), hspec()),
        scratch_shapes=[
            pltpu.SMEM((fields,), jnp.int32),
            pltpu.SMEM((fields,), jnp.int32),
            pltpu.VMEM(pooled.shape, BF),
            pltpu.VMEM(weight.shape, BF),
            pltpu.VMEM((tab, total, owner), BF),
            pltpu.VMEM(pooled.shape, BF),
            pltpu.VMEM((total, slots * padded), BF),
            pltpu.VMEM((total, padded), BF),
            pltpu.SemaphoreType.DMA((4,)),
            pltpu.SemaphoreType.DMA((slots,)),
            pltpu.SemaphoreType.DMA((tab,)),
        ],
        compiler_params=params(14),
        name="slot_grad",
    )(*far(widths, placement, pooled, weight), grads)


def rep_body(*refs):
    parts, small = refs[:-1], refs[-1]
    summed = parts[0][...].astype(F32)
    for part in parts[1:]:
        summed = summed + part[...].astype(F32)
    lines = summed.astype(BF)
    for t in range(small.shape[0]):
        small[t] = lines


def rep_sums(parts, tab):
    return pl.pallas_call(
        rep_body,
        out_shape=jax.ShapeDtypeStruct((tab,) + parts[0].shape, BF),
        in_specs=[vspec()] * len(parts),
        out_specs=vspec(),
        compiler_params=params(4),
        name="rep_sums",
    )(*parts)


def unpack_body(arrived, d_second, d_in, d_out, d_bil, d_last, flat):
    tab, _, lanes = arrived.shape
    hidden = d_second.shape[0]
    lines = flat.shape[0] // tab
    for t in range(tab):
        block = arrived[t].astype(F32)
        for i in range(hidden // lanes):
            flat[t * lines : (t + 1) * lines, i * lanes : (i + 1) * lanes] = block[i * lines : (i + 1) * lines]
    d_second[...] = flat[:hidden, :]
    senet, fields = d_in.shape
    width = d_bil.shape[0]
    band = flat[hidden : hidden + senet, :]
    d_in[...] = band[:, :fields]
    d_out[...] = band[:, fields : 2 * fields]
    d_bil[...] = band[:width, 2 * fields : 2 * fields + width]
    column = 2 * fields + width
    pieces = jnp.concatenate([band[:, column + i : column + i + 1] for i in range(hidden // senet)], axis=0)
    row = lax.broadcasted_iota(jnp.int32, (hidden, hidden), 0)
    across = lax.broadcasted_iota(jnp.int32, (hidden, hidden), 1)
    d_last[...] = jnp.sum(jnp.where(row == across, pieces, 0.0), axis=0, keepdims=True)


def unpack(arrived, hidden, senet, fields, width):
    tab = arrived.shape[0]
    lines = -(-(hidden + senet) // tab)
    shapes = ((hidden, hidden), (senet, fields), (senet, fields), (width, width), (1, hidden))
    return pl.pallas_call(
        unpack_body,
        out_shape=tuple(jax.ShapeDtypeStruct(s, F32) for s in shapes),
        in_specs=[vspec()],
        out_specs=tuple(vspec() for _ in shapes),
        scratch_shapes=[pltpu.VMEM((lines * tab, hidden), F32)],
        compiler_params=params(4),
        name="unpack",
    )(arrived)


def swap(x, axis, size, bit):
    return lax.ppermute(x, axis, [(i, i ^ bit) for i in range(size)])


def shards(pooled, widths, placement, route, labels, proj, senet_in, senet_out, bilinear, w_first, w_second, w_last):
    tab = lax.axis_size("tab")
    rep = lax.axis_size("rep")
    rep_index = lax.axis_index("rep")
    slots, rep_rows, padded = pooled.shape
    fields, senet = senet_in.shape
    width = proj.shape[2]
    owner = rep_rows // tab
    hidden = w_second.shape[0]
    chips = tab // 2

    local, weight = embed_slots(widths, placement, pooled, proj.transpose(0, 2, 1), tab)
    arrived = lax.all_to_all(local, "tab", 0, 0, tiled=True).reshape(fields * width, owner)
    first_turned, second_turned, kron_high, kron_low, back_high, last_column = prepare(
        weight, w_first, w_second, bilinear, w_last.reshape(1, hidden)
    )
    kept, moved, send = owner_pass(
        placement, arrived, labels.reshape(tab, owner), senet_in.T, senet_out, kron_high, kron_low,
        first_turned, second_turned, last_column, w_second, back_high, w_first,
    )
    came = swap(moved, "tab", tab, 1)
    grads = lax.all_to_all(send, "tab", 0, 0, tiled=True)
    parts = first_grad(kept, moved, came)
    rows = parts[0].shape[0]
    sent = [swap(parts[q], "tab", tab, 2 * q) for q in range(1, chips)]

    base = slots * width
    line = hidden // owner * -(-(hidden + senet) // tab)
    small, scores = tab_sums(grads, route.reshape(tab, owner), base, line)
    smalls = [small] + [swap(small, "rep", rep, q) for q in range(1, rep)]
    d_pooled, d_proj = slot_grad(widths, placement, pooled, weight, grads)
    projs = [d_proj] + [swap(d_proj, "rep", rep, q) for q in range(1, rep)]
    proj_sum = sum(p.astype(F32) for p in projs)
    d_proj = proj_sum.reshape(slots, width, padded).transpose(0, 2, 1)
    small = rep_sums(smalls, tab)
    small = lax.all_to_all(small, "tab", 0, 0, tiled=True)
    g_second, g_in, g_out, g_bil, g_last = unpack(small, hidden, senet, fields, width)

    first_sum = parts[0].astype(F32)
    for part in sent:
        first_sum = first_sum + part.astype(F32)
    low_bit = rep_index % 2
    halves = first_sum.astype(BF).reshape(2, rows // 2, hidden)
    mine = lax.dynamic_index_in_dim(halves, low_bit, 0, keepdims=False)
    theirs = lax.dynamic_index_in_dim(halves, 1 - low_bit, 0, keepdims=False)
    theirs = swap(theirs, "rep", rep, 1)
    mine = (mine.astype(F32) + theirs.astype(F32)).astype(BF)
    bit = 2
    while bit < rep:
        theirs = swap(mine, "rep", rep, bit)
        mine = (mine.astype(F32) + theirs.astype(F32)).astype(BF)
        bit *= 2
    back = swap(mine, "rep", rep, 1)
    d_first = jnp.where(
        low_bit == 0, jnp.concatenate([mine, back], axis=0), jnp.concatenate([back, mine], axis=0)
    ).astype(F32)
    return (
        scores, d_pooled, d_proj, g_in.T, g_out, g_bil, d_first, g_second, g_last.reshape(hidden),
    )


def solution(mesh):
    placed = (
        P("tab", "rep", None), P(), P(), P("rep", None), P("rep", None),
        P(), P(), P(), P(), P(), P(), P(),
    )
    return jax.shard_map(
        shards,
        mesh=mesh,
        in_specs=placed,
        out_specs=(P("rep", "tab"), P("tab", "rep", None), P("tab", None, None), P(), P(), P(), P("tab", None), P(), P()),
        check_vma=False,
    )
```

time: 255 us -> 90 us (0.35)
  waiting for transfers between devices: 104 us -> 23.1 us
  blocking collectives: 76.9 us -> 0 us
  Pallas kernels: 0 us -> 28.5 us
  starting transfers between devices: 5.32 us -> 33 us
  matrix products: 25.2 us -> 0 us
  local copies, waits for them, and re-layouts: 19.2 us -> 0.59 us
  between operations: 16 us -> 0.77 us
  other arithmetic: 8.18 us -> 3.59 us
    reduce_scatter x1 -> x0, waiting for transfers between devices: 87.1 us -> none  [shards(): lax.psum_scatter(d_first_part, ('tab', 'rep'), scatter_dimension=0, tiled...]
    psum x1 -> x0, blocking collectives: 41.4 us -> none  [shards(): lax.psum((part_in, part_out, part_bil, part_second, part_last), ('tab', '...]
    pallas_call x0 -> x8, Pallas kernels: none -> 28.5 us  [the longest x1 11 us: owner_pass(): pl.pallas_call(owner_body, out_shape=tuple((pltpu.HBM(s, d) for s, d in s...]
    dot_general x23 -> x0, matrix products: 25.2 us -> none  [the longest x2 4.46 us: bilinear_backward(): jnp.einsum('fnc,fnd->cd', fields_in, d_product, precision=PRECISE)]
    all_gather x2 -> x0, blocking collectives: 22.3 us -> none  [the longest x1 14.3 us: shards(): lax.all_gather(first_all.astype(jnp.bfloat16), 'rep', axis=0, tiled=True)]
    ppermute x0 -> x13, starting transfers between devices: none -> 17 us  [swap(): return lax.ppermute(x, axis, [(i, i ^ bit) for i in range(size)])]
    ppermute x0 -> x13, waiting for transfers between devices: none -> 13.6 us  [swap(): return lax.ppermute(x, axis, [(i, i ^ bit) for i in range(size)])]
    all_to_all x1 -> x0, blocking collectives: 13.1 us -> none  [shards(): lax.all_to_all(d_slot, 'tab', split_axis=0, concat_axis=1, tiled=True)]
  transfers between devices with their start and end apart: 4 -> 16, of which waited for: 3 -> 7; matrix products, arithmetic and copies ran while one was open for 7% -> 4% of each run, Pallas kernels for 0% -> 11%
where the time goes in v1:
time: 90 us; the launch traced here: 89.5 us
  starting transfers between devices  33 us (37%)
  Pallas kernels  28.5 us (32%)
  waiting for transfers between devices  23.1 us (26%)
  other arithmetic  3.59 us (4%)
    ppermute x13, starting transfers between devices, swap(): return lax.ppermute(x, axis, [(i, i ^ bit) for i in range(size)])  17 us
    ppermute x13, waiting for transfers between devices, swap(): return lax.ppermute(x, axis, [(i, i ^ bit) for i in range(size)])  13.6 us
    pallas_call x1, Pallas kernels, owner_pass(): pl.pallas_call(owner_body, out_shape=tuple((pltpu.HBM(s, d) for s, d in s...  11 us
    all_to_all x1, starting transfers between devices, shards(): small = lax.all_to_all(small, 'tab', 0, 0, tiled=True)  7.19 us
    all_to_all x1, waiting for transfers between devices, shards(): lax.all_to_all(local, 'tab', 0, 0, tiled=True)  5.38 us
    all_to_all x1, starting transfers between devices, shards(): lax.all_to_all(local, 'tab', 0, 0, tiled=True)  5.21 us
    pallas_call x1, Pallas kernels, slot_grad(): pl.pallas_call(slot_body, out_shape=(pltpu.HBM(pooled.shape, BF), pltpu.H...  4.22 us
    pallas_call x1, Pallas kernels, embed_slots(): pl.pallas_call(embed_body, out_shape=(pltpu.HBM((tab, slots * width, rows...  4.18 us
  transfers between devices with their start and end apart: 16, of which 7 were waited for; matrix products, arithmetic and copies ran while one was open for 4% of the time, Pallas kernels for 11%

profile of v1, /device:TPU:0, one launch (start us, length us, event | category | flops | bytes accessed | tf_op | source)
XLA Modules:
  0.0 89.5 jit_solution(9326028925680292790)
XLA Ops:
  0.7 4.2 %embed_slots.1 = (bf16[8,256,128]{2,1,0:T(8,128)(2,1)}, bf16[256,128]{1,0:T(8,128)(2,1)}) custom-call(s32[64]{0:T(128)} %widths_hbm.3, s32[64]{0:T(128)} %placement_hbm.5, bf16[8,1024,128]{2,1,0:T(8,128)(2,1)} %pooled.3, bf16[64,32,128]{2,1,0:T(8,128)(2,1)} %bitcast.20), custom_call_target="tpu_custom_call" | custom-call | tf_op jit(solution)/shard_map/embed_slots/pallas_call | solution.py:95
  4.8 5.2 %all-to-all-start = ((bf16[8,256,128]{2,1,0:T(8,128)(2,1)}), bf16[8,256,128]{2,1,0:T(8,128)(2,1)S(1)}, u32[]{:S(2)}, u32[]{:S(2)}) async-start(bf16[8,256,128]{2,1,0:T(8,128)(2,1)} %get-tuple-element.33), calls=%async_computation | async-start | bytes 1048576 | tf_op jit(solution)/shard_map/all_to_all | solution.py:612
  10.6 3.8 %prepare.1 = (bf16[256,4096]{1,0:T(8,128)(2,1)}, bf16[256,256]{1,0:T(8,128)(2,1)}, bf16[256,256]{1,0:T(8,128)(2,1)}, bf16[256,256]{1,0:T(8,128)(2,1)}, bf16[256,256]{1,0:T(8,128)(2,1)}, /*index=5*/f32[256,1]{1,0:T(8,128)}) custom-call(bf16[256,128]{1,0:T(8,128)(2,1)} %get-tuple-element.34.order.weight_hbm, bf16[4096,256]{1,0:T(8,128)(2,1)} %refs_11_.1, ...), custom_call_target="tpu_custom_call" | custom-call | tf_op jit(solution)/shard_map/prepare/pallas_call | solution.py:166
  14.4 5.4 %all-to-all-done = bf16[8,256,128]{2,1,0:T(8,128)(2,1)S(1)} async-done(((bf16[8,256,128]{2,1,0:T(8,128)(2,1)}), bf16[8,256,128]{2,1,0:T(8,128)(2,1)S(1)}, u32[]{:S(2)}, u32[]{:S(2)}) %all-to-all-start) | async-done | bytes 524320 | tf_op jit(solution)/shard_map/all_to_all | solution.py:612
  19.8 11.0 %owner_pass.1 = (bf16[4,512,128]{2,1,0:T(8,128)(2,1)}, bf16[2304,128]{1,0:T(8,128)(2,1)}, bf16[8,336,128]{2,1,0:T(8,128)(2,1)}) custom-call(s32[64]{0:T(128)} %placement_hbm.5, bf16[2048,128]{1,0:T(8,128)(2,1)S(1)} %bitcast.16, s32[8,128]{1,0:T(8,128)} %bitcast.23, f32[32,64]{1,0:T(8,128)} %bitcast.22, f32[32,64]{1,0:T(8,128)} %refs_3_.1, ...), custom_call_target="tpu_custom_call" | custom-call | tf_op jit(solution)/shard_map/owner_pass/pallas_call | solution.py:353
  30.9 2.2 %collective-permute-done.6.came_hbm = bf16[2304,128]{1,0:T(8,128)(2,1)S(1)} collective-permute-done((bf16[2304,128]{1,0:T(8,128)(2,1)}, bf16[2304,128]{1,0:T(8,128)(2,1)S(1)}, u32[]{:S(2)}, u32[]{:S(2)}) %collective-permute-start.6) | collective-permute-done | bytes 589856 | tf_op jit(solution)/shard_map/ppermute | solution.py:597
  33.1 3.1 %first_grad.1 = (bf16[512,256]{1,0:T(8,128)(2,1)}, bf16[512,256]{1,0:T(8,128)(2,1)}, bf16[512,256]{1,0:T(8,128)(2,1)}, bf16[512,256]{1,0:T(8,128)(2,1)}) custom-call(bf16[4,512,128]{2,1,0:T(8,128)(2,1)} %get-tuple-element.49.kept_hbm, bf16[2304,128]{1,0:T(8,128)(2,1)} %get-tuple-element.50.moved_hbm, bf16[2304,128]{1,0:T(8,128)(2,1)S(1)} %collective-permute-done.6.came_hbm), custom_call_target="tpu_custom_call" | custom-call | tf_op jit(solution)/shard_map/first_grad/pallas_call | solution.py:417
  37.3 2.4 %collective-permute-start.9 = (bf16[512,256]{1,0:T(8,128)(2,1)}, bf16[512,256]{1,0:T(8,128)(2,1)S(1)}, u32[]{:S(2)}, u32[]{:S(2)}) collective-permute-start(bf16[512,256]{1,0:T(8,128)(2,1)} %get-tuple-element.54), channel_id=1, source_target_pairs={{0,24},{4,28},{8,16},{12,20},{16,8},{20,12},{24,0},{28,4},{1,25},{... | collective-permute-start | bytes 786440 | tf_op jit(solution)/shard_map/ppermute | solution.py:597
  39.7 3.5 %all-to-all-start.1 = ((bf16[8,336,128]{2,1,0:T(8,128)(2,1)}), bf16[8,336,128]{2,1,0:T(8,128)(2,1)S(1)}, u32[]{:S(2)}, u32[]{:S(2)}) async-start(bf16[8,336,128]{2,1,0:T(8,128)(2,1)} %get-tuple-element.41), calls=%async_computation.1 | async-start | bytes 1376256 | tf_op jit(solution)/shard_map/all_to_all | solution.py:621
  43.2 2.4 %collective-permute-done.7 = bf16[512,256]{1,0:T(8,128)(2,1)S(1)} collective-permute-done((bf16[512,256]{1,0:T(8,128)(2,1)}, bf16[512,256]{1,0:T(8,128)(2,1)S(1)}, u32[]{:S(2)}, u32[]{:S(2)}) %collective-permute-start.7) | collective-permute-done | bytes 262176 | tf_op jit(solution)/shard_map/ppermute | solution.py:597
  45.6 4.8 %collective-permute-done.8 = bf16[512,256]{1,0:T(8,128)(2,1)S(1)} collective-permute-done((bf16[512,256]{1,0:T(8,128)(2,1)}, bf16[512,256]{1,0:T(8,128)(2,1)S(1)}, u32[]{:S(2)}, u32[]{:S(2)}) %collective-permute-start.8) | collective-permute-done | bytes 262176 | tf_op jit(solution)/shard_map/ppermute | solution.py:597
  51.3 1.1 %add_convert_fusion = bf16[512,256]{1,0:T(8,128)(2,1)S(1)} fusion(bf16[512,256]{1,0:T(8,128)(2,1)S(1)} %collective-permute-done.9, bf16[512,256]{1,0:T(8,128)(2,1)S(1)} %collective-permute-done.8, bf16[512,256]{1,0:T(8,128)(2,1)S(1)} %collective-permute-done.7, bf16[512,256]{1,0:T(8,128)(2,1)} %get-tuple-element.51), kind=kLoop, calls=%fused_computation | loop fusion | flops 1048576 | bytes 1310720 | tf_op jit(solution)/shard_map/convert_element_type | solution.py:642
  52.4 1.6 %collective-permute-start.10 = (bf16[256,256]{1,0:T(8,128)(2,1)S(1)}, bf16[256,256]{1,0:T(8,128)(2,1)S(1)}, u32[]{:S(2)}, u32[]{:S(2)}) collective-permute-start(bf16[256,256]{1,0:T(8,128)(2,1)S(1)} %dynamic-slice_bitcast_fusion), channel_id=1, source_target_pairs={{0,1},{1,0},{2,3},{3,2},{4,5},{5,4},{6,7},{7,6},{8,9},{9,8},{10,11... | collective-permute-start | bytes 393224 | tf_op jit(solution)/shard_map/ppermute | solution.py:597
  54.0 3.4 %collective-permute-done.10 = bf16[256,256]{1,0:T(8,128)(2,1)S(1)} collective-permute-done((bf16[256,256]{1,0:T(8,128)(2,1)S(1)}, bf16[256,256]{1,0:T(8,128)(2,1)S(1)}, u32[]{:S(2)}, u32[]{:S(2)}) %collective-permute-start.10) | collective-permute-done | bytes 131104 | tf_op jit(solution)/shard_map/ppermute | solution.py:597
  57.5 2.7 %collective-permute-start.11 = (bf16[256,256]{1,0:T(8,128)(2,1)S(1)}, bf16[256,256]{1,0:T(8,128)(2,1)S(1)}, u32[]{:S(2)}, u32[]{:S(2)}) collective-permute-start(bf16[256,256]{1,0:T(8,128)(2,1)S(1)} %fusion.1), channel_id=1, source_target_pairs={{0,2},{1,3},{2,0},{3,1},{4,6},{5,7},{6,4},{7,5},{8,10},{9,11},{10,... | collective-permute-start | bytes 393224 | tf_op jit(solution)/shard_map/ppermute | solution.py:597
  60.9 1.6 %collective-permute-start.3 = (bf16[80,128]{1,0:T(8,128)(2,1)S(1)}, bf16[80,128]{1,0:T(8,128)(2,1)S(1)}, u32[]{:S(2)}, u32[]{:S(2)}) collective-permute-start(bf16[80,128]{1,0:T(8,128)(2,1)S(1)} %get-tuple-element.45.refs_0_), channel_id=1, source_target_pairs={{0,1},{1,0},{2,3},{3,2},{4,5},{5,4},{6,7},{7,6},{8,9},{9,8},{10,11... | collective-permute-start | bytes 61448 | tf_op jit(solution)/shard_map/ppermute | solution.py:597
  63.0 2.3 %collective-permute-start.5 = (bf16[80,128]{1,0:T(8,128)(2,1)S(1)}, bf16[80,128]{1,0:T(8,128)(2,1)S(1)}, u32[]{:S(2)}, u32[]{:S(2)}) collective-permute-start(bf16[80,128]{1,0:T(8,128)(2,1)S(1)} %get-tuple-element.45.refs_0_), channel_id=1, source_target_pairs={{0,3},{1,2},{2,1},{3,0},{4,7},{5,6},{6,5},{7,4},{8,11},{9,10},{10,... | collective-permute-start | bytes 61448 | tf_op jit(solution)/shard_map/ppermute | solution.py:597
  65.3 4.2 %slot_grad.1 = (bf16[8,1024,128]{2,1,0:T(8,128)(2,1)}, bf16[256,128]{1,0:T(8,128)(2,1)}) custom-call(s32[64]{0:T(128)} %widths_hbm.3, s32[64]{0:T(128)} %placement_hbm.5, bf16[8,1024,128]{2,1,0:T(8,128)(2,1)} %pooled.3, bf16[256,128]{1,0:T(8,128)(2,1)} %get-tuple-element.34.order.weight_hbm, bf16[8,336,128]{2,1,0:T(8,128)(2,1)S(1)} %all-to-all-done.1.grads_any), custom_call_target="tpu_custom_call" | custom-call | tf_op jit(solution)/shard_map/slot_grad/pallas_call | solution.py:515
  70.3 1.4 %collective-permute-start.1 = (bf16[256,128]{1,0:T(8,128)(2,1)}, bf16[256,128]{1,0:T(8,128)(2,1)S(1)}, u32[]{:S(2)}, u32[]{:S(2)}) collective-permute-start(bf16[256,128]{1,0:T(8,128)(2,1)} %get-tuple-element.44), channel_id=1, source_target_pairs={{0,2},{1,3},{2,0},{3,1},{4,6},{5,7},{6,4},{7,5},{8,10},{9,11},{10,... | collective-permute-start | bytes 196616 | tf_op jit(solution)/shard_map/ppermute | solution.py:597
  71.7 2.3 %collective-permute-start.2 = (bf16[256,128]{1,0:T(8,128)(2,1)}, bf16[256,128]{1,0:T(8,128)(2,1)S(1)}, u32[]{:S(2)}, u32[]{:S(2)}) collective-permute-start(bf16[256,128]{1,0:T(8,128)(2,1)} %get-tuple-element.44), channel_id=1, source_target_pairs={{0,3},{1,2},{2,1},{3,0},{4,7},{5,6},{6,5},{7,4},{8,11},{9,10},{10,... | collective-permute-start | bytes 196616 | tf_op jit(solution)/shard_map/ppermute | solution.py:597
  74.7 7.2 %all-to-all-start.2 = ((bf16[8,80,128]{2,1,0:T(8,128)(2,1)}), bf16[8,80,128]{2,1,0:T(8,128)(2,1)S(1)}, u32[]{:S(2)}, u32[]{:S(2)}) async-start(bf16[8,80,128]{2,1,0:T(8,128)(2,1)} %rep_sums.1), calls=%async_computation.2 | async-start | bytes 327680 | tf_op jit(solution)/shard_map/all_to_all | solution.py:635
  82.2 1.5 %convert_add_fusion.1 = f32[256,128]{1,0:T(8,128)} fusion(bf16[256,128]{1,0:T(8,128)(2,1)S(1)} %collective-permute-done.2, bf16[256,128]{1,0:T(8,128)(2,1)S(1)} %collective-permute-done.1, bf16[256,128]{1,0:T(8,128)(2,1)S(1)} %collective-permute-done, bf16[256,128]{1,0:T(8,128)(2,1)} %get-tuple-element.44), kind=kLoop, calls=%fused_computation.7 | loop fusion | flops 229376 | bytes 393216 | tf_op jit(solution)/shard_map/add | solution.py:632
  83.7 4.0 %all-to-all-done.2.arrived = bf16[8,80,128]{2,1,0:T(8,128)(2,1)S(1)} async-done(((bf16[8,80,128]{2,1,0:T(8,128)(2,1)}), bf16[8,80,128]{2,1,0:T(8,128)(2,1)S(1)}, u32[]{:S(2)}, u32[]{:S(2)}) %all-to-all-start.2) | async-done | bytes 163872 | tf_op jit(solution)/shard_map/all_to_all | solution.py:635
  88.6 0.9 fusion
  (27 shorter events, 6.5 us)
Async XLA Ops:
  0.6 9.4 %copy-start.1 = (bf16[256]{0:T(256)(128)(2,1)S(1)}, bf16[256]{0:T(256)(128)(2,1)}, u32[]{:S(2)}) copy-start(bf16[256]{0:T(256)(128)(2,1)} %param.23) | copy-start | bytes 1540
  4.8 14.9 %all-to-all-start = ((bf16[8,256,128]{2,1,0:T(8,128)(2,1)}), bf16[8,256,128]{2,1,0:T(8,128)(2,1)S(1)}, u32[]{:S(2)}, u32[]{:S(2)}) async-start(bf16[8,256,128]{2,1,0:T(8,128)(2,1)} %get-tuple-element.33), calls=%async_computation | async-start | bytes 1048576 | tf_op jit(solution)/shard_map/all_to_all | solution.py:612
  30.8 2.3 %collective-permute-start.6 = (bf16[2304,128]{1,0:T(8,128)(2,1)}, bf16[2304,128]{1,0:T(8,128)(2,1)S(1)}, u32[]{:S(2)}, u32[]{:S(2)}) collective-permute-start(bf16[2304,128]{1,0:T(8,128)(2,1)} %get-tuple-element.50.moved_hbm), channel_id=1, source_target_pairs={{0,4},{4,0},{8,12},{12,8},{16,20},{20,16},{24,28},{28,24},{1,5},{5... | collective-permute-start | bytes 1769480 | tf_op jit(solution)/shard_map/ppermute | solution.py:597
  36.1 24.0 %copy-start = (s32[1,1024]{1,0:T(1,128)S(1)}, s32[1,1024]{1,0:T(1,128)}, u32[]{:S(2)}) copy-start(s32[1,1024]{1,0:T(1,128)} %param.15) | copy-start | bytes 12292
  36.1 9.5 %collective-permute-start.7 = (bf16[512,256]{1,0:T(8,128)(2,1)}, bf16[512,256]{1,0:T(8,128)(2,1)S(1)}, u32[]{:S(2)}, u32[]{:S(2)}) collective-permute-start(bf16[512,256]{1,0:T(8,128)(2,1)} %get-tuple-element.52), channel_id=1, source_target_pairs={{0,8},{4,12},{8,0},{12,4},{16,24},{20,28},{24,16},{28,20},{1,9},{5... | collective-permute-start | bytes 786440 | tf_op jit(solution)/shard_map/ppermute | solution.py:597
  36.8 13.7 %collective-permute-start.8 = (bf16[512,256]{1,0:T(8,128)(2,1)}, bf16[512,256]{1,0:T(8,128)(2,1)S(1)}, u32[]{:S(2)}, u32[]{:S(2)}) collective-permute-start(bf16[512,256]{1,0:T(8,128)(2,1)} %get-tuple-element.53), channel_id=1, source_target_pairs={{0,16},{4,20},{8,24},{12,28},{16,0},{20,4},{24,8},{28,12},{1,17},{... | collective-permute-start | bytes 786440 | tf_op jit(solution)/shard_map/ppermute | solution.py:597
  37.3 13.9 %collective-permute-start.9 = (bf16[512,256]{1,0:T(8,128)(2,1)}, bf16[512,256]{1,0:T(8,128)(2,1)S(1)}, u32[]{:S(2)}, u32[]{:S(2)}) collective-permute-start(bf16[512,256]{1,0:T(8,128)(2,1)} %get-tuple-element.54), channel_id=1, source_target_pairs={{0,24},{4,28},{8,16},{12,20},{16,8},{20,12},{24,0},{28,4},{1,25},{... | collective-permute-start | bytes 786440 | tf_op jit(solution)/shard_map/ppermute | solution.py:597
  39.7 20.4 %all-to-all-start.1 = ((bf16[8,336,128]{2,1,0:T(8,128)(2,1)}), bf16[8,336,128]{2,1,0:T(8,128)(2,1)S(1)}, u32[]{:S(2)}, u32[]{:S(2)}) async-start(bf16[8,336,128]{2,1,0:T(8,128)(2,1)} %get-tuple-element.41), calls=%async_computation.1 | async-start | bytes 1376256 | tf_op jit(solution)/shard_map/all_to_all | solution.py:621
  52.4 5.0 %collective-permute-start.10 = (bf16[256,256]{1,0:T(8,128)(2,1)S(1)}, bf16[256,256]{1,0:T(8,128)(2,1)S(1)}, u32[]{:S(2)}, u32[]{:S(2)}) collective-permute-start(bf16[256,256]{1,0:T(8,128)(2,1)S(1)} %dynamic-slice_bitcast_fusion), channel_id=1, source_target_pairs={{0,1},{1,0},{2,3},{3,2},{4,5},{5,4},{6,7},{7,6},{8,9},{9,8},{10,11... | collective-permute-start | bytes 393224 | tf_op jit(solution)/shard_map/ppermute | solution.py:597
  57.5 24.4 %collective-permute-start.11 = (bf16[256,256]{1,0:T(8,128)(2,1)S(1)}, bf16[256,256]{1,0:T(8,128)(2,1)S(1)}, u32[]{:S(2)}, u32[]{:S(2)}) collective-permute-start(bf16[256,256]{1,0:T(8,128)(2,1)S(1)} %fusion.1), channel_id=1, source_target_pairs={{0,2},{1,3},{2,0},{3,1},{4,6},{5,7},{6,4},{7,5},{8,10},{9,11},{10,... | collective-permute-start | bytes 393224 | tf_op jit(solution)/shard_map/ppermute | solution.py:597
  60.9 9.4 %collective-permute-start.3 = (bf16[80,128]{1,0:T(8,128)(2,1)S(1)}, bf16[80,128]{1,0:T(8,128)(2,1)S(1)}, u32[]{:S(2)}, u32[]{:S(2)}) collective-permute-start(bf16[80,128]{1,0:T(8,128)(2,1)S(1)} %get-tuple-element.45.refs_0_), channel_id=1, source_target_pairs={{0,1},{1,0},{2,3},{3,2},{4,5},{5,4},{6,7},{7,6},{8,9},{9,8},{10,11... | collective-permute-start | bytes 61448 | tf_op jit(solution)/shard_map/ppermute | solution.py:597
  62.5 9.2 %collective-permute-start.4 = (bf16[80,128]{1,0:T(8,128)(2,1)S(1)}, bf16[80,128]{1,0:T(8,128)(2,1)S(1)}, u32[]{:S(2)}, u32[]{:S(2)}) collective-permute-start(bf16[80,128]{1,0:T(8,128)(2,1)S(1)} %get-tuple-element.45.refs_0_), channel_id=1, source_target_pairs={{0,2},{1,3},{2,0},{3,1},{4,6},{5,7},{6,4},{7,5},{8,10},{9,11},{10,... | collective-permute-start | bytes 61448 | tf_op jit(solution)/shard_map/ppermute | solution.py:597
  63.0 11.0 %collective-permute-start.5 = (bf16[80,128]{1,0:T(8,128)(2,1)S(1)}, bf16[80,128]{1,0:T(8,128)(2,1)S(1)}, u32[]{:S(2)}, u32[]{:S(2)}) collective-permute-start(bf16[80,128]{1,0:T(8,128)(2,1)S(1)} %get-tuple-element.45.refs_0_), channel_id=1, source_target_pairs={{0,3},{1,2},{2,1},{3,0},{4,7},{5,6},{6,5},{7,4},{8,11},{9,10},{10,... | collective-permute-start | bytes 61448 | tf_op jit(solution)/shard_map/ppermute | solution.py:597
  69.6 12.6 %collective-permute-start = (bf16[256,128]{1,0:T(8,128)(2,1)}, bf16[256,128]{1,0:T(8,128)(2,1)S(1)}, u32[]{:S(2)}, u32[]{:S(2)}) collective-permute-start(bf16[256,128]{1,0:T(8,128)(2,1)} %get-tuple-element.44), channel_id=1, source_target_pairs={{0,1},{1,0},{2,3},{3,2},{4,5},{5,4},{6,7},{7,6},{8,9},{9,8},{10,11... | collective-permute-start | bytes 196616 | tf_op jit(solution)/shard_map/ppermute | solution.py:597
  70.3 11.9 %collective-permute-start.1 = (bf16[256,128]{1,0:T(8,128)(2,1)}, bf16[256,128]{1,0:T(8,128)(2,1)S(1)}, u32[]{:S(2)}, u32[]{:S(2)}) collective-permute-start(bf16[256,128]{1,0:T(8,128)(2,1)} %get-tuple-element.44), channel_id=1, source_target_pairs={{0,2},{1,3},{2,0},{3,1},{4,6},{5,7},{6,4},{7,5},{8,10},{9,11},{10,... | collective-permute-start | bytes 196616 | tf_op jit(solution)/shard_map/ppermute | solution.py:597
  71.7 10.4 %collective-permute-start.2 = (bf16[256,128]{1,0:T(8,128)(2,1)}, bf16[256,128]{1,0:T(8,128)(2,1)S(1)}, u32[]{:S(2)}, u32[]{:S(2)}) collective-permute-start(bf16[256,128]{1,0:T(8,128)(2,1)} %get-tuple-element.44), channel_id=1, source_target_pairs={{0,3},{1,2},{2,1},{3,0},{4,7},{5,6},{6,5},{7,4},{8,11},{9,10},{10,... | collective-permute-start | bytes 196616 | tf_op jit(solution)/shard_map/ppermute | solution.py:597
  74.7 13.0 %all-to-all-start.2 = ((bf16[8,80,128]{2,1,0:T(8,128)(2,1)}), bf16[8,80,128]{2,1,0:T(8,128)(2,1)S(1)}, u32[]{:S(2)}, u32[]{:S(2)}) async-start(bf16[8,80,128]{2,1,0:T(8,128)(2,1)} %rep_sums.1), calls=%async_computation.2 | async-start | bytes 327680 | tf_op jit(solution)/shard_map/all_to_all | solution.py:635
  82.0 6.6 %collective-permute-start.12 = (bf16[256,256]{1,0:T(8,128)(2,1)S(1)}, bf16[256,256]{1,0:T(8,128)(2,1)S(1)}, u32[]{:S(2)}, u32[]{:S(2)}) collective-permute-start(bf16[256,256]{1,0:T(8,128)(2,1)S(1)} %add_convert_fusion.1), channel_id=1, source_target_pairs={{0,1},{1,0},{2,3},{3,2},{4,5},{5,4},{6,7},{7,6},{8,9},{9,8},{10,11... | collective-permute-start | bytes 393224 | tf_op jit(solution)/shard_map/ppermute | solution.py:597
